TPU v7x, 32 devices: a whole 2x2x4 slice. The times are simulated.
32 devices in a mesh: owner: 8 (over y, x, core), rows: 4 (over z).
Axes of the slice: x: 2, y: 2, z: 4, core: 2. Of those that a mesh axis runs over, the one named last changes fastest.
Arguments:
- w_down: float32 [64, 1024, 2048], P('owner', None, 'rows'), may hold values from -0.1875 to 0.1875
- router_weight: float32 [2048, 64], P('rows', 'owner'), may hold values from -0.125 to 0.125
- router_gain: float32 [2048], P('rows'), may hold values from 0.25 to 1.75
Outputs:
- serve_down: bfloat16 [64, 2048, 1024], P('owner')
- serve_router: bfloat16 [2048, 64], replicated
All inputs are finite; a program needn't handle non-finite values.
Results may differ from a plain program's by a relative error of at most 0.001.
Values may be sent and summed in bfloat16 or wider, within the bound.
A program may use at most 128 MiB of HBM per device.

v0:
```python
import jax
import jax.numpy as jnp
from jax import lax
from jax.sharding import PartitionSpec as P


def shards(w_down, router_weight, router_gain):
    narrow_down = w_down.astype(jnp.bfloat16)
    serve_down = lax.all_gather(narrow_down, "rows", axis=2, tiled=True)
    serve_down = jnp.transpose(serve_down, (0, 2, 1))
    part_router = (router_weight * router_gain[:, None]).astype(jnp.bfloat16)
    row_router = lax.all_gather(part_router, "rows", axis=0, tiled=True)
    serve_router = lax.all_gather(row_router, "owner", axis=1, tiled=True)
    return (serve_down, serve_router)


def solution(mesh):
    in_specs = (P("owner", None, "rows"), P("rows", "owner"), P("rows"))
    out_specs = (P("owner", None, None), P())
    return jax.shard_map(shards, mesh=mesh, in_specs=in_specs, out_specs=out_specs, check_vma=False)
```

profile of v0, /device:TPU:0, one launch (start us, length us, event | category | flops | bytes accessed | tf_op | source)
XLA Modules:
  0.0 615.9 jit_solution(6089209621411756597)
XLA Ops:
  7.2 0.0 copy-start
  7.2 0.0 copy-start.1
  7.2 0.0 all-gather.2.cloned.1.call-start
  7.2 13.6 %copy.5 = bf16[8,1024,512]{1,2,0:T(8,128)(2,1)} copy(f32[8,1024,512]{2,1,0:T(8,128)} %param.3) | data formatting | bytes 25165824 | tf_op args[0]
  20.8 0.0 all-gather.2.cloned.1.call-update
  20.8 0.0 copy-done
  20.8 0.0 copy-done.1
  20.9 14.8 %all_gather.10 = bf16[2048,8]{0,1:T(8,128)(2,1)S(1)} all-gather(bf16[512,8]{0,1:T(8,128)(2,1)S(1)} %multiply_convert_fusion), channel_id=1, replica_groups=mesh['owner'=8,'rows'=4] {'rows'}, dimensions={0}, use_global_device_ids=true | all-gather | bytes 40960 | tf_op jit(solution)/shard_map/all_gather | solution.py:12
  35.7 9.3 %all_gather.11 = bf16[2048,64]{0,1:T(8,128)(2,1)S(1)} all-gather(bf16[2048,8]{0,1:T(8,128)(2,1)S(1)} %all_gather.10), channel_id=1, replica_groups=mesh['owner'=8,'rows'=4] {'owner'}, dimensions={1}, use_global_device_ids=true | all-gather | bytes 294912 | tf_op jit(solution)/shard_map/all_gather | solution.py:13
  45.0 540.1 %all-gather.2.cloned.1.call-done = bf16[8,1024,2048]{1,2,0:T(8,128)(2,1)} async-done(((bf16[8,1024,512]{1,2,0:T(8,128)(2,1)}), bf16[8,1024,2048]{1,2,0:T(8,128)(2,1)}) %all-gather.2.cloned.1.call-update) | async-done | bytes 33554448 | tf_op jit(solution)/shard_map/all_gather | solution.py:9
  585.1 23.2 %copy.8 = bf16[8,2048,1024]{2,1,0:T(8,128)(2,1)} copy(bf16[8,2048,1024]{2,1,0:T(8,128)(2,1)} %bitcast.1) | data formatting | bytes 67108864
  608.3 0.7 copy.9
  (1 shorter events, 0.0 us)
Async XLA Ops:
  7.2 13.7 %copy-start = (f32[512,8]{0,1:T(8,128)S(1)}, f32[512,8]{0,1:T(8,128)}, u32[]{:S(2)}) copy-start(f32[512,8]{0,1:T(8,128)} %param.4) | copy-start | bytes 49156
  7.2 13.7 %copy-start.1 = (f32[512]{0:T(512)S(1)}, f32[512]{0:T(512)}, u32[]{:S(2)}) copy-start(f32[512]{0:T(512)} %param.5) | copy-start | bytes 6148
  7.2 577.9 %all-gather.2.cloned.1.call-start = ((), (), s32[]{:S(2)}) async-start(), calls=%async_computation | async-start | bytes 41943040 | tf_op jit(solution)/shard_map/all_gather | solution.py:9
Sparse Core Ops, SparseCore 0:
  20.9 564.0 all-gather.1
where the time goes:
time: 616 us
  waiting for transfers between devices  540 us (88%)
  local copies, waits for them, and re-layouts  37.5 us (6%)
  blocking collectives  24.1 us (4%)
  between operations  14.1 us (2%)
    all_gather x1, waiting for transfers between devices, shards(): serve_down = lax.all_gather(narrow_down, 'rows', axis=2, tiled=True)  540 us
    unnamed x7, local copies, waits for them, and re-layouts  37.5 us
    all_gather x1, blocking collectives, shards(): row_router = lax.all_gather(part_router, 'rows', axis=0, tiled=True)  14.8 us
  transfers between devices with their start and end apart: 1, of which 1 were waited for; matrix products, arithmetic and copies ran while one was open for 0% of the time, Pallas kernels for 0%

commit v1 on v0

--- a/solution.py
+++ b/solution.py
@@ -6,7 +6,7 @@
 
 def shards(w_down, router_weight, router_gain):
     narrow_down = w_down.astype(jnp.bfloat16)
-    serve_down = lax.all_gather(narrow_down, "rows", axis=2, tiled=True)
+    serve_down = jnp.concatenate(lax.all_gather(narrow_down, "rows"), axis=2)
     serve_down = jnp.transpose(serve_down, (0, 2, 1))
     part_router = (router_weight * router_gain[:, None]).astype(jnp.bfloat16)
     row_router = lax.all_gather(part_router, "rows", axis=0, tiled=True)

time: 616 us -> 631 us (1.024)
  other arithmetic: 0.01 us -> 8.98 us
    reshape x0 -> x1, local copies, waits for them, and re-layouts: none -> 42 us  [shards(): serve_down = jnp.concatenate(lax.all_gather(narrow_down, 'rows'), axis=2)]
    unnamed x7 -> x5, local copies, waits for them, and re-layouts: 37.5 us -> 0.71 us
    convert_element_type x0 -> x1, other arithmetic: none -> 8.98 us  [shards(): narrow_down = w_down.astype(jnp.bfloat16)]
where the time goes in v1:
time: 631 us; the launch traced here: 630 us
  waiting for transfers between devices  540 us (86%)
  local copies, waits for them, and re-layouts  42.7 us (7%)
  blocking collectives  24.1 us (4%)
  between operations  14.1 us (2%)
  other arithmetic  8.98 us (1%)
    all_gather x1, waiting for transfers between devices, shards(): serve_down = jnp.concatenate(lax.all_gather(narrow_down, 'rows'), axis=2)  540 us
    reshape x1, local copies, waits for them, and re-layouts, shards(): serve_down = jnp.concatenate(lax.all_gather(narrow_down, 'rows'), axis=2)  42 us
    all_gather x1, blocking collectives, shards(): row_router = lax.all_gather(part_router, 'rows', axis=0, tiled=True)  14.8 us
  transfers between devices with their start and end apart: 1, of which 1 were waited for; matrix products, arithmetic and copies ran while one was open for 0% of the time, Pallas kernels for 0%

profile of v1, /device:TPU:0, one launch (start us, length us, event | category | flops | bytes accessed | tf_op | source)
XLA Modules:
  0.0 630.0 jit_solution(4098347636613212321)
XLA Ops:
  7.2 0.0 copy-start
  7.2 0.0 copy-start.1
  7.2 0.0 all-gather.3.cloned.1.call-start
  7.2 9.0 %convert_element_type.6 = bf16[8,1024,512]{2,1,0:T(8,128)(2,1)} convert(f32[8,1024,512]{2,1,0:T(8,128)} %param.3) | non-fusion elementwise | flops 4194304 | bytes 25165824 | tf_op jit(solution)/shard_map/convert_element_type | solution.py:8
  16.2 0.0 all-gather.3.cloned.1.call-update
  16.2 0.0 copy-done
  16.2 0.0 copy-done.1
  16.3 14.8 %all_gather.14 = bf16[2048,8]{0,1:T(8,128)(2,1)S(1)} all-gather(bf16[512,8]{0,1:T(8,128)(2,1)S(1)} %multiply_convert_fusion), channel_id=1, replica_groups=mesh['owner'=8,'rows'=4] {'rows'}, dimensions={0}, use_global_device_ids=true | all-gather | bytes 40960 | tf_op jit(solution)/shard_map/all_gather | solution.py:12
  31.1 9.3 %all_gather.15 = bf16[2048,64]{0,1:T(8,128)(2,1)S(1)} all-gather(bf16[2048,8]{0,1:T(8,128)(2,1)S(1)} %all_gather.14), channel_id=1, replica_groups=mesh['owner'=8,'rows'=4] {'owner'}, dimensions={1}, use_global_device_ids=true | all-gather | bytes 294912 | tf_op jit(solution)/shard_map/all_gather | solution.py:13
  40.4 540.1 %all-gather.3.cloned.1.call-done = bf16[32,1024,512]{2,1,0:T(8,128)(2,1)} async-done(((bf16[8,1024,512]{2,1,0:T(8,128)(2,1)}), bf16[32,1024,512]{2,1,0:T(8,128)(2,1)}) %all-gather.3.cloned.1.call-update) | async-done | bytes 33554448 | tf_op jit(solution)/shard_map/all_gather | solution.py:9
  580.5 42.0 %copy.6 = bf16[8,1024,4,512]{1,3,2,0:T(8,128)(2,1)} copy(bf16[8,1024,4,512]{3,1,0,2:T(8,128)(2,1)} %bitcast.6) | data formatting | bytes 67108864 | tf_op jit(solution)/shard_map/reshape | solution.py:9
  622.5 0.7 copy.8
  (1 shorter events, 0.0 us)
Async XLA Ops:
  7.2 9.1 %copy-start = (f32[512,8]{0,1:T(8,128)S(1)}, f32[512,8]{0,1:T(8,128)}, u32[]{:S(2)}) copy-start(f32[512,8]{0,1:T(8,128)} %param.4) | copy-start | bytes 49156
  7.2 9.1 %copy-start.1 = (f32[512]{0:T(512)S(1)}, f32[512]{0:T(512)}, u32[]{:S(2)}) copy-start(f32[512]{0:T(512)} %param.5) | copy-start | bytes 6148
  7.2 573.3 %all-gather.3.cloned.1.call-start = ((), (), s32[]{:S(2)}) async-start(), calls=%async_computation | async-start | bytes 41943040 | tf_op jit(solution)/shard_map/all_gather | solution.py:9
Sparse Core Ops, SparseCore 0:
  16.4 564.0 all-gather.2
